TPU v7x, 32 devices: a whole 2x2x4 slice. The times are simulated.
32 devices in a mesh: grp: 2 (over x), rep: 8 (over z, y), blk: 2 (over core).
Axes of the slice: x: 2, y: 2, z: 4, core: 2. Of those that a mesh axis runs over, the one named last changes fastest.
Arguments:
- factors: float32 [16, 1280, 1280], P('grp', ('blk', 'rep')), as said below
- damping: float32 [16], P('grp'), may hold values from 0.1 to 1
Outputs:
- root: float32 [16, 1280, 1280], P('grp', ('blk', 'rep'))
- inv_root: float32 [16, 1280, 1280], P('grp', ('blk', 'rep'))
Inputs may be any that keep to these rules, and one draw needn't show every extreme that they name: `factors`: every factor is symmetric positive semidefinite.
All inputs are finite; a program needn't handle non-finite values.
Results may differ from a plain program's by a relative error of at most 0.0035.
The roundings to bfloat16 on the way count: a program that leaves them out, or rounds other values in their place, can miss the bound.
Values may be sent and summed in bfloat16 or wider, within the bound.
A program may use at most 128 MiB of HBM per device.

v0:
```python
import jax
import jax.numpy as jnp
from jax import lax
from jax.sharding import PartitionSpec as P

ITERS = 4


def per_device(factors, damping):
    fac_grp = factors.shape[0]
    row_count = factors.shape[1]
    order_full = factors.shape[2]
    rep_count = lax.axis_size("rep")
    fac_rep = fac_grp // rep_count
    blk_rows = row_count * rep_count
    blk_idx = lax.axis_index("blk")
    rep_idx = lax.axis_index("rep")
    row_ids = blk_idx * blk_rows + rep_idx * row_count + lax.iota(jnp.int32, row_count)
    col_ids = lax.iota(jnp.int32, order_full)
    eye_block = (row_ids[:, None] == col_ids[None, :]).astype(jnp.float32)
    damped = factors + damping[:, None, None] * eye_block[None, :, :]
    factor_norms = jnp.sqrt(lax.psum(jnp.sum(damped * damped, axis=(1, 2)), ("rep", "blk")))
    own_rows = lax.all_to_all(damped, "rep", split_axis=0, concat_axis=1, tiled=True)
    own_norms = lax.dynamic_slice_in_dim(factor_norms, rep_idx * fac_rep, fac_rep)
    iterate = (own_rows / own_norms[:, None, None]).astype(jnp.bfloat16)
    iter_rows = blk_idx * blk_rows + lax.iota(jnp.int32, blk_rows)
    eye_rows = (iter_rows[:, None] == col_ids[None, :]).astype(jnp.float32)
    inverse = eye_rows[None, :, :].astype(jnp.bfloat16)
    for sweep_idx in range(ITERS):
        whole_iter, whole_inv = (
            lax.all_gather(iterate, "blk", axis=1, tiled=True),
            lax.all_gather(inverse, "blk", axis=1, tiled=True),
        )
        eye_full = jnp.eye(order_full, dtype=jnp.float32)
        moment_full = jnp.einsum(
            "fik,fkj->fij", whole_inv, whole_iter, preferred_element_type=jnp.float32
        )
        step_full = ((3.0 * eye_full[None, :, :] - moment_full) * 0.5).astype(jnp.bfloat16)
        step_rows = lax.dynamic_slice_in_dim(step_full, blk_idx * blk_rows, blk_rows, 1)
        new_iterate = jnp.einsum(
            "fik,fkj->fij", iterate, step_full, preferred_element_type=jnp.float32
        )
        new_inverse = jnp.einsum(
            "fik,fkj->fij", step_rows, whole_inv, preferred_element_type=jnp.float32
        )
        iterate = new_iterate.astype(jnp.bfloat16)
        inverse = new_inverse.astype(jnp.bfloat16)
    root_block, inv_block = (
        lax.all_to_all(iterate, "rep", split_axis=1, concat_axis=0, tiled=True),
        lax.all_to_all(inverse, "rep", split_axis=1, concat_axis=0, tiled=True),
    )
    root_scale = jnp.sqrt(factor_norms)[:, None, None]
    return (root_block.astype(jnp.float32) * root_scale, inv_block.astype(jnp.float32) / root_scale)


def solution(mesh):
    return jax.shard_map(
        per_device,
        mesh=mesh,
        in_specs=(P("grp", ("blk", "rep"), None), P("grp")),
        out_specs=(P("grp", ("blk", "rep"), None), P("grp", ("blk", "rep"), None)),
        check_vma=False,
    )
```

profile of v0, /device:TPU:0, one launch (start us, length us, event | category | flops | bytes accessed | tf_op | source)
XLA Modules:
  0.0 384.2 jit_solution(16059342983351797581)
XLA Ops:
  7.2 0.1 fusion.21
  7.3 4.3 %multiply_reduce_fusion = (f32[8]{0:T(128)S(1)}, f32[8,80,1280]{2,1,0:T(8,128)}) fusion(f32[8,80,1280]{2,1,0:T(8,128)} %param.2, f32[80,1280]{1,0:T(8,128)S(1)} %fusion.21, f32[8]{0:T(128)} %param.3), kind=kLoop, calls=%fused_computation.20 | loop fusion | flops 3276792 | bytes 6963264 | tf_op jit(solution)/shard_map/reduce_sum | solution.py:22
  11.6 7.3 %all-to-all-start = ((f32[8,80,1280]{2,1,0:T(8,128)}), f32[8,80,1280]{2,1,0:T(8,128)S(1)}, u32[]{:S(2)}, u32[]{:S(2)}) async-start(f32[8,80,1280]{2,1,0:T(8,128)} %get-tuple-element.3), calls=%async_computation | async-start | bytes 6553600 | tf_op jit(solution)/shard_map/all_to_all | solution.py:23
  18.9 0.0 all-gather.15.cloned.1.call-start
  19.0 1.5 convert_convert_fusion
  20.5 0.0 all-gather.15.cloned.1.call-update
  20.5 0.0 all-gather.17.cloned.1.call-start
  20.5 80.0 %psum.7 = f32[8]{0:T(128)S(1)} all-reduce(f32[8]{0:T(128)S(1)} %get-tuple-element.2), channel_id=1, replica_groups=mesh['grp'=2,'rep'=8,'blk'=2] {'rep','blk'}, use_global_device_ids=true, to_apply=%region_1.0 | all-reduce | flops 8 | bytes 64 | tf_op jit(solution)/shard_map/psum | solution.py:22
  100.6 0.6 dynamic_slice.2
  101.2 2.0 divide_convert_fusion
  103.2 0.0 all-gather.17.cloned.1.call-update
  103.2 0.0 all-gather.21.cloned.1.call-start
  103.3 0.0 all-gather.15.cloned.1.call-done
  103.3 20.4 %all-gather.17.cloned.1.call-done = bf16[1,1280,1280]{2,1,0:T(8,128)(2,1)} async-done(((bf16[1,640,1280]{2,1,0:T(8,128)(2,1)}), bf16[1,1280,1280]{2,1,0:T(8,128)(2,1)}) %all-gather.17.cloned.1.call-update) | async-done | bytes 3276816 | tf_op jit(solution)/shard_map/all_gather | solution.py:31
  123.7 7.3 %fusion.4 = bf16[1280,1280]{1,0:T(8,128)(2,1)S(1)} fusion(bf16[1,1280,1280]{2,1,0:T(8,128)(2,1)} %all-gather.17.cloned.1.call-done, bf16[1,1280,1280]{2,1,0:T(8,128)(2,1)} %all-gather.15.cloned.1.call-done), kind=kOutput, calls=%fused_computation.8 | convolution fusion | flops 4202496000 | bytes 9830400 | tf_op jit(solution)/shard_map/fik,fkj->fij/dot_general | solution.py:35
  131.1 1.7 copy-done.5
  132.8 3.5 convolution_convert_fusion.6
  136.3 0.0 all-gather.21.cloned.1.call-update
  136.3 0.0 all-gather.19.cloned.1.call-start
  136.4 5.9 %fusion.12 = bf16[640,1280]{1,0:T(8,128)(2,1)} fusion(bf16[1,1280,1280]{2,1,0:T(8,128)(2,1)} %all-gather.15.cloned.1.call-done, bf16[1280,1280]{1,0:T(8,128)(2,1)} %copy-done.5, s32[]{:T(128)S(6)} %select_n.10), kind=kOutput, calls=%fused_computation.22 | convolution fusion | flops 2097971200 | bytes 6553604 | tf_op jit(solution)/shard_map/fik,fkj->fij/dot_general | solution.py:43
  142.3 0.0 all-gather.19.cloned.1.call-update
  142.3 0.2 all-gather.25.cloned.1.call-start
  142.5 7.5 %all-gather.21.cloned.1.call-done = bf16[1280,1280]{1,0:T(8,128)(2,1)} async-done(((bf16[640,1280]{1,0:T(8,128)(2,1)}), bf16[1280,1280]{1,0:T(8,128)(2,1)}) %all-gather.21.cloned.1.call-update) | async-done | bytes 3276816 | tf_op jit(solution)/shard_map/all_gather | solution.py:31
  150.0 15.5 %all-gather.19.cloned.1.call-done = bf16[1280,1280]{1,0:T(8,128)(2,1)} async-done(((bf16[640,1280]{1,0:T(8,128)(2,1)}), bf16[1280,1280]{1,0:T(8,128)(2,1)}) %all-gather.19.cloned.1.call-update) | async-done | bytes 3276816 | tf_op jit(solution)/shard_map/all_gather | solution.py:32
  165.5 7.3 %fusion.5 = bf16[1280,1280]{1,0:T(8,128)(2,1)S(1)} fusion(bf16[1280,1280]{1,0:T(8,128)(2,1)} %all-gather.19.cloned.1.call-done, bf16[1280,1280]{1,0:T(8,128)(2,1)} %all-gather.21.cloned.1.call-done), kind=kOutput, calls=%fused_computation.9 | convolution fusion | flops 4202496000 | bytes 9830400 | tf_op jit(solution)/shard_map/fik,fkj->fij/dot_general | solution.py:35
  172.8 0.0 copy-start.7
  172.8 1.7 copy-done.7
  174.5 3.5 convolution_convert_fusion.5
  178.0 0.0 all-gather.25.cloned.1.call-update
  178.1 0.0 all-gather.23.cloned.1.call-start
  178.1 5.9 %convolution_convert_fusion.4 = bf16[640,1280]{1,0:T(8,128)(2,1)} fusion(bf16[1280,1280]{1,0:T(8,128)(2,1)} %all-gather.19.cloned.1.call-done, bf16[1280,1280]{1,0:T(8,128)(2,1)} %copy-done.7, s32[]{:T(128)S(6)} %select_n.10), kind=kOutput, calls=%fused_computation.27 | convolution fusion | flops 2097971200 | bytes 6553604 | tf_op jit(solution)/shard_map/fik,fkj->fij/dot_general | solution.py:43
  184.0 0.0 all-gather.23.cloned.1.call-update
  184.0 0.0 all-gather.29.cloned.1.call-start
  184.1 7.6 %all-gather.25.cloned.1.call-done = bf16[1280,1280]{1,0:T(8,128)(2,1)} async-done(((bf16[640,1280]{1,0:T(8,128)(2,1)}), bf16[1280,1280]{1,0:T(8,128)(2,1)}) %all-gather.25.cloned.1.call-update) | async-done | bytes 3276816 | tf_op jit(solution)/shard_map/all_gather | solution.py:31
  191.7 15.5 %all-gather.23.cloned.1.call-done = bf16[1280,1280]{1,0:T(8,128)(2,1)} async-done(((bf16[640,1280]{1,0:T(8,128)(2,1)}), bf16[1280,1280]{1,0:T(8,128)(2,1)}) %all-gather.23.cloned.1.call-update) | async-done | bytes 3276816 | tf_op jit(solution)/shard_map/all_gather | solution.py:32
  207.2 7.3 %fusion.6 = bf16[1280,1280]{1,0:T(8,128)(2,1)S(1)} fusion(bf16[1280,1280]{1,0:T(8,128)(2,1)} %all-gather.23.cloned.1.call-done, bf16[1280,1280]{1,0:T(8,128)(2,1)} %all-gather.25.cloned.1.call-done), kind=kOutput, calls=%fused_computation.10 | convolution fusion | flops 4202496000 | bytes 9830400 | tf_op jit(solution)/shard_map/fik,fkj->fij/dot_general | solution.py:35
  214.5 0.0 copy-start.8
  214.5 1.7 copy-done.8
  216.2 3.5 convolution_convert_fusion.3
  219.8 0.0 all-gather.29.cloned.1.call-update
  219.8 0.3 all-gather.27.cloned.1.call-start
  220.0 5.9 %convolution_convert_fusion.2 = bf16[640,1280]{1,0:T(8,128)(2,1)} fusion(bf16[1280,1280]{1,0:T(8,128)(2,1)} %all-gather.23.cloned.1.call-done, bf16[1280,1280]{1,0:T(8,128)(2,1)} %copy-done.8, s32[]{:T(128)S(6)} %select_n.10), kind=kOutput, calls=%fused_computation.25 | convolution fusion | flops 2097971200 | bytes 6553604 | tf_op jit(solution)/shard_map/fik,fkj->fij/dot_general | solution.py:43
  225.9 0.0 all-gather.27.cloned.1.call-update
  226.0 7.5 %all-gather.29.cloned.1.call-done = bf16[1280,1280]{1,0:T(8,128)(2,1)} async-done(((bf16[640,1280]{1,0:T(8,128)(2,1)}), bf16[1280,1280]{1,0:T(8,128)(2,1)}) %all-gather.29.cloned.1.call-update) | async-done | bytes 3276816 | tf_op jit(solution)/shard_map/all_gather | solution.py:31
  233.4 15.6 %all-gather.27.cloned.1.call-done = bf16[1280,1280]{1,0:T(8,128)(2,1)} async-done(((bf16[640,1280]{1,0:T(8,128)(2,1)}), bf16[1280,1280]{1,0:T(8,128)(2,1)}) %all-gather.27.cloned.1.call-update) | async-done | bytes 3276816 | tf_op jit(solution)/shard_map/all_gather | solution.py:32
  249.1 7.3 %fusion.7 = bf16[1280,1280]{1,0:T(8,128)(2,1)S(1)} fusion(bf16[1280,1280]{1,0:T(8,128)(2,1)} %all-gather.27.cloned.1.call-done, bf16[1280,1280]{1,0:T(8,128)(2,1)} %all-gather.29.cloned.1.call-done), kind=kOutput, calls=%fused_computation.11 | convolution fusion | flops 4202496000 | bytes 9830400 | tf_op jit(solution)/shard_map/fik,fkj->fij/dot_general | solution.py:35
  256.4 2.3 fusion.15
  258.7 2.5 copy.11
  261.3 0.6 broadcast.81
  261.9 12.2 %reduce.1 = bf16[640,1280]{1,0:T(8,128)(2,1)} reduce(bf16[640,1,1280]{2,1,0:T(2,128)(2,1)S(1)} %bitcast.46, bf16[]{:T(256)} %broadcast.81), dimensions={1}, to_apply=%bitcast.43.reduce_sub_computation | reduce | bytes 3276802
  274.1 3.9 %reshape.220 = bf16[8,2,51200]{2,1,0:T(2,128)(2,1)} reshape(bf16[640,1280]{1,0:T(8,128)(2,1)} %reduce.1) | data formatting | bytes 3276800
  278.0 5.9 %all-to-all-start.1 = ((bf16[8,2,51200]{2,1,0:T(2,128)(2,1)}), bf16[8,2,51200]{2,1,0:T(2,128)(2,1)}, u32[]{:S(2)}, u32[]{:S(2)}) async-start(bf16[8,2,51200]{2,1,0:T(2,128)(2,1)} %reshape.220), calls=%async_computation.1 | async-start | bytes 3276800 | tf_op jit(solution)/shard_map/all_to_all | solution.py:49
  284.0 3.7 fusion.16
  287.7 2.5 copy.10
  290.2 12.1 %reduce = bf16[640,1280]{1,0:T(8,128)(2,1)} reduce(bf16[640,1,1280]{2,1,0:T(2,128)(2,1)S(1)} %bitcast.47, bf16[]{:T(256)} %broadcast.81), dimensions={1}, to_apply=%bitcast.42.reduce_sub_computation | reduce | bytes 3276802
  302.3 3.7 reshape.222
  306.0 16.8 %all-to-all-done.1 = bf16[8,2,51200]{2,1,0:T(2,128)(2,1)} async-done(((bf16[8,2,51200]{2,1,0:T(2,128)(2,1)}), bf16[8,2,51200]{2,1,0:T(2,128)(2,1)}, u32[]{:S(2)}, u32[]{:S(2)}) %all-to-all-start.1) | async-done | bytes 1638432 | tf_op jit(solution)/shard_map/all_to_all | solution.py:49
  322.8 4.3 %all-to-all-start.2 = ((bf16[8,2,51200]{2,1,0:T(2,128)(2,1)}), bf16[8,2,51200]{2,1,0:T(2,128)(2,1)}, u32[]{:S(2)}, u32[]{:S(2)}) async-start(bf16[8,2,51200]{2,1,0:T(2,128)(2,1)} %reshape.222), calls=%async_computation.2 | async-start | bytes 3276800 | tf_op jit(solution)/shard_map/all_to_all | solution.py:50
  327.1 6.4 %reshape.221 = bf16[640,1,1280]{2,1,0:T(2,128)(2,1)} reshape(bf16[8,2,51200]{2,1,0:T(2,128)(2,1)} %all-to-all-done.1) | data formatting | bytes 3276800
  333.5 2.1 copy.6
  335.6 29.5 %all-to-all-done.2 = bf16[8,2,51200]{2,1,0:T(2,128)(2,1)} async-done(((bf16[8,2,51200]{2,1,0:T(2,128)(2,1)}), bf16[8,2,51200]{2,1,0:T(2,128)(2,1)}, u32[]{:S(2)}, u32[]{:S(2)}) %all-to-all-start.2) | async-done | bytes 1638432 | tf_op jit(solution)/shard_map/all_to_all | solution.py:50
  365.1 6.4 %reshape.223 = bf16[640,1,1280]{2,1,0:T(2,128)(2,1)} reshape(bf16[8,2,51200]{2,1,0:T(2,128)(2,1)} %all-to-all-done.2) | data formatting | bytes 3276800
  371.5 2.1 copy.7
  373.6 3.5 broadcast_divide_fusion
  (17 shorter events, 0.1 us)
Async XLA Ops:
  11.6 89.6 %all-to-all-start = ((f32[8,80,1280]{2,1,0:T(8,128)}), f32[8,80,1280]{2,1,0:T(8,128)S(1)}, u32[]{:S(2)}, u32[]{:S(2)}) async-start(f32[8,80,1280]{2,1,0:T(8,128)} %get-tuple-element.3), calls=%async_computation | async-start | bytes 6553600 | tf_op jit(solution)/shard_map/all_to_all | solution.py:23
  18.9 84.4 %all-gather.15.cloned.1.call-start = ((), (), s32[]{:S(2)}) async-start(), calls=%async_computation.3 | async-start | bytes 4915200 | tf_op jit(solution)/shard_map/all_gather | solution.py:32
  20.5 103.3 %all-gather.17.cloned.1.call-start = ((), (), s32[]{:S(2)}) async-start(), calls=%async_computation.4 | async-start | bytes 4915200 | tf_op jit(solution)/shard_map/all_gather | solution.py:31
  103.2 29.6 %copy-start = (bf16[8,80,1280]{2,1,0:T(8,128)(2,1)S(1)}, bf16[8,80,1280]{2,1,0:T(8,128)(2,1)}, u32[]{:S(2)}) copy-start(bf16[8,80,1280]{2,1,0:T(8,128)(2,1)} %divide_convert_fusion) | copy-start | bytes 4915204
  103.2 46.7 %all-gather.21.cloned.1.call-start = ((), (), s32[]{:S(2)}) async-start(), calls=%async_computation.6 | async-start | bytes 4915200 | tf_op jit(solution)/shard_map/all_gather | solution.py:31
  131.1 1.7 copy-start.5
  136.3 29.1 %all-gather.19.cloned.1.call-start = ((), (), s32[]{:S(2)}) async-start(), calls=%async_computation.5 | async-start | bytes 4915200 | tf_op jit(solution)/shard_map/all_gather | solution.py:32
  142.3 32.2 %copy-start.1 = (bf16[640,1280]{1,0:T(8,128)(2,1)S(1)}, bf16[640,1280]{1,0:T(8,128)(2,1)}, u32[]{:S(2)}) copy-start(bf16[640,1280]{1,0:T(8,128)(2,1)} %convolution_convert_fusion.6) | copy-start | bytes 4915204
  142.3 49.4 %all-gather.25.cloned.1.call-start = ((), (), s32[]{:S(2)}) async-start(), calls=%async_computation.8 | async-start | bytes 4915200 | tf_op jit(solution)/shard_map/all_gather | solution.py:31
  172.8 1.7 copy-start.7
  178.1 29.1 %all-gather.23.cloned.1.call-start = ((), (), s32[]{:S(2)}) async-start(), calls=%async_computation.7 | async-start | bytes 4915200 | tf_op jit(solution)/shard_map/all_gather | solution.py:32
  184.0 32.2 %copy-start.2 = (bf16[640,1280]{1,0:T(8,128)(2,1)S(1)}, bf16[640,1280]{1,0:T(8,128)(2,1)}, u32[]{:S(2)}) copy-start(bf16[640,1280]{1,0:T(8,128)(2,1)} %convolution_convert_fusion.5) | copy-start | bytes 4915204
  184.0 49.4 %all-gather.29.cloned.1.call-start = ((), (), s32[]{:S(2)}) async-start(), calls=%async_computation.10 | async-start | bytes 4915200 | tf_op jit(solution)/shard_map/all_gather | solution.py:31
  214.5 1.7 copy-start.8
  219.8 29.3 %all-gather.27.cloned.1.call-start = ((), (), s32[]{:S(2)}) async-start(), calls=%async_computation.9 | async-start | bytes 4915200 | tf_op jit(solution)/shard_map/all_gather | solution.py:32
  225.9 30.5 %copy-start.3 = (bf16[640,1280]{1,0:T(8,128)(2,1)S(1)}, bf16[640,1280]{1,0:T(8,128)(2,1)}, u32[]{:S(2)}) copy-start(bf16[640,1280]{1,0:T(8,128)(2,1)} %convolution_convert_fusion.3) | copy-start | bytes 4915204
  256.4 2.3 copy-start.6
  274.1 9.9 %copy-start.4 = (bf16[1280,1280]{1,0:T(8,128)(2,1)S(1)}, bf16[1280,1280]{1,0:T(8,128)(2,1)}, u32[]{:S(2)}) copy-start(bf16[1280,1280]{1,0:T(8,128)(2,1)} %all-gather.27.cloned.1.call-done) | copy-start | bytes 9830404
  278.0 44.8 %all-to-all-start.1 = ((bf16[8,2,51200]{2,1,0:T(2,128)(2,1)}), bf16[8,2,51200]{2,1,0:T(2,128)(2,1)}, u32[]{:S(2)}, u32[]{:S(2)}) async-start(bf16[8,2,51200]{2,1,0:T(2,128)(2,1)} %reshape.220), calls=%async_computation.1 | async-start | bytes 3276800 | tf_op jit(solution)/shard_map/all_to_all | solution.py:49
  322.8 42.3 %all-to-all-start.2 = ((bf16[8,2,51200]{2,1,0:T(2,128)(2,1)}), bf16[8,2,51200]{2,1,0:T(2,128)(2,1)}, u32[]{:S(2)}, u32[]{:S(2)}) async-start(bf16[8,2,51200]{2,1,0:T(2,128)(2,1)} %reshape.222), calls=%async_computation.2 | async-start | bytes 3276800 | tf_op jit(solution)/shard_map/all_to_all | solution.py:50
Sparse Core Ops, SparseCore 0:
  21.8 13.7 all-gather.14
  103.3 20.3 all-gather.16
  136.4 13.4 all-gather.20
  151.9 13.4 all-gather.18
  178.2 13.4 all-gather.24
  193.7 13.4 all-gather.22
  219.9 13.4 all-gather.28
  235.5 13.4 all-gather.26
where the time goes:
time: 391 us; the launch traced here: 384 us
  waiting for transfers between devices  136 us (35%)
  blocking collectives  80 us (20%)
  matrix products  63.5 us (16%)
  local copies, waits for them, and re-layouts  36.1 us (9%)
  other arithmetic  35.8 us (9%)
  starting transfers between devices  18.3 us (5%)
  between operations  14.6 us (4%)
    psum x1, blocking collectives, per_device(): lax.psum(jnp.sum(damped * damped, axis=(1, 2)), ('rep', 'blk'))  80 us
    all_gather x4, waiting for transfers between devices, per_device(): lax.all_gather(inverse, 'blk', axis=1, tiled=True)  46.7 us
    all_gather x4, waiting for transfers between devices, per_device(): lax.all_gather(iterate, 'blk', axis=1, tiled=True)  43 us
    unnamed x25, local copies, waits for them, and re-layouts  30.4 us
    all_to_all x1, waiting for transfers between devices, per_device(): lax.all_to_all(inverse, 'rep', split_axis=1, concat_axis=0, tiled=True)  29.5 us
    dot_general x4, matrix products, per_device(): jnp.einsum('fik,fkj->fij', whole_inv, whole_iter, preferred_element_type=...  29.3 us
    unnamed x2, other arithmetic  24.3 us
    dot_general x4, matrix products, per_device(): jnp.einsum('fik,fkj->fij', step_rows, whole_inv, preferred_element_type=j...  21.3 us
  transfers between devices with their start and end apart: 11, of which 9 were waited for; matrix products, arithmetic and copies ran while one was open for 14% of the time, Pallas kernels for 0%

commit v1 on v0

v1 whole, which is shorter than its diff:
```python
import functools

import jax
import jax.numpy as jnp
from jax import lax
from jax.experimental import pallas as pl
from jax.experimental.pallas import tpu as pltpu
from jax.sharding import PartitionSpec as P

ITERS = 4
LANES = 128
CHUNK = 256
MESH = pl.DeviceIdType.MESH


def kernel(
    reps, fac_hbm, damp_ref,
    root_ref, inv_ref, norm_ref,
    fac, part, scale, send_buf, full, step, last_root,
    load_sem, sum_send, sum_recv, in_send, in_recv, fwd_send, fwd_recv,
    ex_send, ex_recv, root_send, root_recv, inv_send, inv_recv,
):
    grp = lax.axis_index("grp")
    rep = lax.axis_index("rep")
    blk = lax.axis_index("blk")
    facs, rows, order = fac.shape
    half = rows * reps
    members = 2 * reps
    rank = blk * reps + rep
    chunks = order // CHUNK
    f32, bf16 = jnp.float32, jnp.bfloat16

    def remote(src, dst, send, recv, r, b):
        return pltpu.make_async_remote_copy(
            src_ref=src, dst_ref=dst, send_sem=send, recv_sem=recv,
            device_id=(grp, r, b), device_id_type=MESH,
        )

    def member(j):
        q = lax.rem(rank + j, members)
        return lax.rem(q, reps), q // reps

    loads = [
        pltpu.make_async_copy(fac_hbm.at[f], fac.at[f], load_sem.at[f]) for f in range(facs)
    ]
    for load in loads:
        load.start()
    barrier = pltpu.get_barrier_semaphore()
    for j in range(1, members):
        r, b = member(j)
        pl.semaphore_signal(barrier, inc=1, device_id=(grp, r, b), device_id_type=MESH)

    row_ids = rank * rows + lax.broadcasted_iota(jnp.int32, (rows, order), 0)
    diag = row_ids == lax.broadcasted_iota(jnp.int32, (rows, order), 1)

    def damped(f):
        return fac[f] + jnp.where(diag, damp_ref[f], 0.0)

    for f in range(facs):
        loads[f].wait()
        x = damped(f)
        col = jnp.sum(x * x, axis=0, keepdims=True)
        acc = col[:, :LANES]
        for c in range(1, order // LANES):
            acc = acc + col[:, c * LANES : (c + 1) * LANES]
        part[pl.ds(rank, 1), f : f + 1, :] = acc[None]
    pl.semaphore_wait(barrier, members - 1)

    sums = []
    for j in range(1, members):
        r, b = member(j)
        copy = remote(part.at[rank], part.at[rank], sum_send.at[j], sum_recv.at[j], r, b)
        copy.start()
        sums.append(copy)
    for copy in sums:
        copy.wait()
    total = part[0]
    for q in range(1, members):
        total = total + part[q]
    norm = jnp.sqrt(jnp.sum(total, axis=1, keepdims=True))
    norm_ref[...] = jnp.broadcast_to(norm, norm_ref.shape)
    scale[...] = jnp.broadcast_to(1.0 / norm, scale.shape)

    y0, z1 = full.at[0], full.at[1]

    def block_rows(b, r):
        return pl.ds(pl.multiple_of((b * reps + r) * rows, rows), rows)

    ins = []
    for k in range(1, reps):
        p = lax.rem(rep + k, reps)
        send_buf[k] = (damped(p) * scale[pl.ds(p, 1), 0:1]).astype(bf16)
        copy = remote(
            send_buf.at[k], y0.at[block_rows(blk, rep)], in_send.at[k], in_recv.at[k], p, blk
        )
        copy.start()
        ins.append(copy)
    y0[block_rows(blk, rep), :] = (damped(rep) * scale[pl.ds(rep, 1), 0:1]).astype(bf16)

    def first_step(b, r):
        at = block_rows(b, r)
        ids = (b * reps + r) * rows + lax.broadcasted_iota(jnp.int32, (rows, order), 0)
        eye = ids == lax.broadcasted_iota(jnp.int32, (rows, order), 1)
        z1[at, :] = ((jnp.where(eye, 3.0, 0.0) - y0[at, :].astype(f32)) * 0.5).astype(bf16)

    forwards = []
    for k in range(reps):
        src = lax.rem(rep - k + reps, reps)
        if k:
            ins[k - 1].wait_recv()
        at = block_rows(blk, src)
        copy = remote(y0.at[at], y0.at[at], fwd_send.at[k], fwd_recv.at[k], rep, 1 - blk)
        copy.start()
        forwards.append(copy)
        first_step(blk, src)
    for k in range(reps):
        src = lax.rem(rep - k + reps, reps)
        forwards[k].wait_recv()
        first_step(1 - blk, src)

    mine = pl.ds(pl.multiple_of(blk * half, half), half)
    pending = []

    def cols(n):
        return slice(n * CHUNK, (n + 1) * CHUNK)

    def share(dst, ex, n):
        view = dst.at[mine, pl.ds(n * CHUNK, CHUNK)]
        copy = remote(view, view, ex_send.at[ex, n], ex_recv.at[ex, n], rep, 1 - blk)
        copy.start()
        pending.append(copy)
        return copy

    def product(lhs, rhs, arrivals, n):
        if arrivals is not None:
            arrivals[n].wait_recv()
        return jnp.dot(lhs, rhs[:, cols(n)], preferred_element_type=f32)

    def advance(lhs, rhs, arrivals, dst, ex):
        shared = []
        for n in range(chunks):
            dst[mine, cols(n)] = product(lhs[...], rhs, arrivals, n).astype(bf16)
            shared.append(share(dst, ex, n))
        return shared

    eye_rows = blk * half + lax.broadcasted_iota(jnp.int32, (half, CHUNK), 0)
    eye_cols = lax.broadcasted_iota(jnp.int32, (half, CHUNK), 1)

    def make_step(y, z, arrivals):
        for n in range(chunks):
            moment = product(y[mine, :], z, arrivals, n)
            eye = jnp.where(eye_rows == eye_cols + n * CHUNK, 3.0, 0.0)
            step[:, cols(n)] = ((eye - moment) * 0.5).astype(bf16)

    y, z, z_in = full.at[2], z1, None
    y_in = advance(z1.at[mine], y0, None, y, 0)
    slot, ex = 3, 1
    for _ in range(ITERS - 2):
        make_step(y, z, z_in)
        z_next, y_next = full.at[slot], full.at[slot + 1]
        z_in_next = advance(step, z, None, z_next, ex)
        y_in = advance(step, y, y_in, y_next, ex + 1)
        y, z, z_in = y_next, z_next, z_in_next
        slot, ex = slot + 2, ex + 2
    make_step(y, z, z_in)

    my_cols = pl.ds(pl.multiple_of(blk * half, LANES), half)
    for n in range(chunks):
        out = product(step[...], y, y_in, n)
        last_root[cols(n), :] = out.T.astype(bf16)
    roots = []
    for j in range(1, members):
        r, b = member(j)
        copy = remote(
            last_root.at[block_rows(b, r)], root_ref.at[rep, :, my_cols],
            root_send.at[j], root_recv.at[j], r, b,
        )
        copy.start()
        roots.append(copy)
    root_ref[rep, :, my_cols] = last_root[block_rows(blk, rep), :]

    for n in range(chunks):
        z1[0:half, cols(n)] = product(step[...], z, None, n).astype(bf16)

    def local_rows(r):
        return pl.ds(pl.multiple_of(r * rows, rows), rows)

    invs = []
    for k in range(1, reps):
        p = lax.rem(rep + k, reps)
        copy = remote(
            z1.at[local_rows(p)], inv_ref.at[rep], inv_send.at[k], inv_recv.at[k], p, blk
        )
        copy.start()
        invs.append(copy)
    inv_ref[rep] = z1[local_rows(rep), :]

    for copy in ins + forwards + pending:
        copy.wait_send()
    for copy in roots + invs:
        copy.wait()


def fused(mesh, factors, damping):
    facs, rows, order = factors.shape
    reps = mesh.shape["rep"]
    members = 2 * reps
    half = rows * reps
    chunks = order // CHUNK
    dma = pltpu.SemaphoreType.DMA
    vmem = pl.BlockSpec(memory_space=pltpu.VMEM)
    exchanges = 2 * ITERS - 3
    root, inv, norm = pl.pallas_call(
        functools.partial(kernel, reps),
        out_shape=(
            jax.ShapeDtypeStruct(factors.shape, jnp.bfloat16),
            jax.ShapeDtypeStruct(factors.shape, jnp.bfloat16),
            jax.ShapeDtypeStruct((facs, LANES), jnp.float32),
        ),
        in_specs=[
            pl.BlockSpec(memory_space=pl.ANY),
            pl.BlockSpec(memory_space=pltpu.SMEM),
        ],
        out_specs=(vmem, vmem, vmem),
        scratch_shapes=[
            pltpu.VMEM(factors.shape, jnp.float32),
            pltpu.VMEM((members, facs, LANES), jnp.float32),
            pltpu.VMEM((facs, LANES), jnp.float32),
            pltpu.VMEM(factors.shape, jnp.bfloat16),
            pltpu.VMEM((2 * ITERS - 1, order, order), jnp.bfloat16),
            pltpu.VMEM((half, order), jnp.bfloat16),
            pltpu.VMEM((order, half), jnp.bfloat16),
            dma((facs,)),
            dma((members,)), dma((members,)),
            dma((reps,)), dma((reps,)),
            dma((reps,)), dma((reps,)),
            dma((exchanges, chunks)), dma((exchanges, chunks)),
            dma((members,)), dma((members,)),
            dma((reps,)), dma((reps,)),
        ],
        compiler_params=pltpu.CompilerParams(
            collective_id=0, has_side_effects=True, vmem_limit_bytes=60 * 2**20
        ),
    )(factors, damping)
    root_scale = jnp.sqrt(norm[:, :1])[:, :, None]
    return root.astype(jnp.float32) * root_scale, inv.astype(jnp.float32) / root_scale


def plain(factors, damping):
    fac_grp, row_count, order_full = factors.shape
    rep_count = lax.axis_size("rep")
    fac_rep = fac_grp // rep_count
    blk_rows = row_count * rep_count
    blk_idx = lax.axis_index("blk")
    rep_idx = lax.axis_index("rep")
    row_ids = blk_idx * blk_rows + rep_idx * row_count + lax.iota(jnp.int32, row_count)
    col_ids = lax.iota(jnp.int32, order_full)
    eye_block = (row_ids[:, None] == col_ids[None, :]).astype(jnp.float32)
    damped = factors + damping[:, None, None] * eye_block[None, :, :]
    factor_norms = jnp.sqrt(lax.psum(jnp.sum(damped * damped, axis=(1, 2)), ("rep", "blk")))
    own_rows = lax.all_to_all(damped, "rep", split_axis=0, concat_axis=1, tiled=True)
    own_norms = lax.dynamic_slice_in_dim(factor_norms, rep_idx * fac_rep, fac_rep)
    iterate = (own_rows / own_norms[:, None, None]).astype(jnp.bfloat16)
    iter_rows = blk_idx * blk_rows + lax.iota(jnp.int32, blk_rows)
    eye_rows = (iter_rows[:, None] == col_ids[None, :]).astype(jnp.float32)
    inverse = eye_rows[None, :, :].astype(jnp.bfloat16)
    for _ in range(ITERS):
        whole_iter = lax.all_gather(iterate, "blk", axis=1, tiled=True)
        whole_inv = lax.all_gather(inverse, "blk", axis=1, tiled=True)
        eye_full = jnp.eye(order_full, dtype=jnp.float32)
        moment = jnp.einsum(
            "fik,fkj->fij", whole_inv, whole_iter, preferred_element_type=jnp.float32
        )
        step = ((3.0 * eye_full[None, :, :] - moment) * 0.5).astype(jnp.bfloat16)
        step_rows = lax.dynamic_slice_in_dim(step, blk_idx * blk_rows, blk_rows, 1)
        new_iterate = jnp.einsum("fik,fkj->fij", iterate, step, preferred_element_type=jnp.float32)
        new_inverse = jnp.einsum(
            "fik,fkj->fij", step_rows, whole_inv, preferred_element_type=jnp.float32
        )
        iterate = new_iterate.astype(jnp.bfloat16)
        inverse = new_inverse.astype(jnp.bfloat16)
    root = lax.all_to_all(iterate, "rep", split_axis=1, concat_axis=0, tiled=True)
    inv = lax.all_to_all(inverse, "rep", split_axis=1, concat_axis=0, tiled=True)
    root_scale = jnp.sqrt(factor_norms)[:, None, None]
    return root.astype(jnp.float32) * root_scale, inv.astype(jnp.float32) / root_scale


def solution(mesh):
    def per_device(factors, damping):
        facs, rows, order = factors.shape
        if (
            facs == mesh.shape["rep"]
            and mesh.shape["blk"] == 2
            and rows % 16 == 0
            and order % CHUNK == 0
        ):
            return fused(mesh, factors, damping)
        return plain(factors, damping)

    return jax.shard_map(
        per_device,
        mesh=mesh,
        in_specs=(P("grp", ("blk", "rep"), None), P("grp")),
        out_specs=(P("grp", ("blk", "rep"), None), P("grp", ("blk", "rep"), None)),
        check_vma=False,
    )
```

time: 391 us -> 170 us (0.43)
  the two profiles are of different devices: /device:TPU:0 before, /device:TPU:31 now
where the time goes in v1:
time: 170 us
  Pallas kernels  163 us (96%)
  other arithmetic  5.48 us (3%)
    pallas_call x1, Pallas kernels, fused(): pl.pallas_call(functools.partial(kernel, reps), out_shape=(jax.ShapeDtype...  163 us
    div x1, other arithmetic, fused(): inv.astype(jnp.float32) / root_scale  5.48 us

profile of v1, /device:TPU:31, one launch (start us, length us, event | category | flops | bytes accessed | tf_op | source)
XLA Modules:
  0.0 170.0 jit_solution(15879577843296919847)
XLA Ops:
  0.6 163.1 %shard_map.41 = (bf16[8,80,1280]{2,1,0:T(8,128)(2,1)}, bf16[8,80,1280]{2,1,0:T(8,128)(2,1)}, f32[8,128]{1,0:T(8,128)}) custom-call(f32[8,80,1280]{2,1,0:T(8,128)} %fac_hbm.1, f32[8]{0:T(128)} %damp_ref.1), custom_call_target="tpu_custom_call" | custom-call | tf_op jit(solution)/shard_map/pallas_call | solution.py:213
  163.8 0.8 sqrt_reduce_fusion
  164.6 5.5 %convert_divide_fusion = (f32[8,80,1280]{2,1,0:T(8,128)}, f32[8,80,1280]{2,1,0:T(8,128)}) fusion(bf16[8,80,1280]{2,1,0:T(8,128)(2,1)} %get-tuple-element.7, f32[8]{0:T(128)S(1)} %sqrt_reduce_fusion, bf16[8,80,1280]{2,1,0:T(8,128)(2,1)} %get-tuple-element.5), kind=kLoop, calls=%fused_computation | loop fusion | flops 3276800 | bytes 9830432 | tf_op jit(solution)/shard_map/div | solution.py:246

commit v2 on v1

--- a/solution.py
+++ b/solution.py
@@ -86,37 +86,90 @@
     def block_rows(b, r):
         return pl.ds(pl.multiple_of((b * reps + r) * rows, rows), rows)
 
+    side_reps = reps // 2
+    side = rep // side_reps
+    wide = -(-(half // 2) // LANES) * LANES
+    narrow = half - wide
+
+    def target(k):
+        if k <= side_reps:
+            return (1 - side) * side_reps + lax.rem(rep + k, side_reps)
+        return side * side_reps + lax.rem(rep + k, side_reps)
+
+    def source(k):
+        if k == 0:
+            return rep
+        back = lax.rem(rep - k + reps, side_reps)
+        if k <= side_reps:
+            return (1 - side) * side_reps + back
+        return side * side_reps + back
+
+    def pieces(k, owner_side):
+        if k == 0 or k > side_reps:
+            return [pl.ds(0, order)]
+        first = (1 - owner_side) * narrow
+        return [
+            pl.ds(pl.multiple_of(h * half + first, LANES), wide) for h in range(2)
+        ]
+
     ins = []
     for k in range(1, reps):
-        p = lax.rem(rep + k, reps)
+        p = target(k)
         send_buf[k] = (damped(p) * scale[pl.ds(p, 1), 0:1]).astype(bf16)
-        copy = remote(
-            send_buf.at[k], y0.at[block_rows(blk, rep)], in_send.at[k], in_recv.at[k], p, blk
-        )
-        copy.start()
-        ins.append(copy)
+        at = block_rows(blk, rep)
+        copies = [
+            remote(
+                send_buf.at[k, :, c], y0.at[at, c],
+                in_send.at[k, i], in_recv.at[k, i], p, blk,
+            )
+            for i, c in enumerate(pieces(k, 1 - side))
+        ]
+        for copy in copies:
+            copy.start()
+        ins.append(copies)
     y0[block_rows(blk, rep), :] = (damped(rep) * scale[pl.ds(rep, 1), 0:1]).astype(bf16)
 
-    def first_step(b, r):
-        at = block_rows(b, r)
-        ids = (b * reps + r) * rows + lax.broadcasted_iota(jnp.int32, (rows, order), 0)
+    forwards = []
+    for k in [0] + list(range(side_reps + 1, reps)) + list(range(1, side_reps + 1)):
+        at = block_rows(blk, source(k))
+        for i, c in enumerate(pieces(k, side)):
+            if k:
+                ins[k - 1][i].wait_recv()
+            copy = remote(
+                y0.at[at, c], y0.at[at, c], fwd_send.at[k, i], fwd_recv.at[k, i], rep, 1 - blk
+            )
+            copy.start()
+            forwards.append(copy)
+    for copy in forwards:
+        copy.wait_recv()
+    for copy in forwards:
+        copy.wait_send()
+
+    far = half // 2
+
+    @pl.when(side == 0)
+    def _():
+        for hi in range(2):
+            for hj in range(2):
+                t = y0[hj * half : hj * half + narrow, hi * half + narrow : (hi + 1) * half]
+                y0[hi * half + far : (hi + 1) * half, hj * half : hj * half + narrow] = (
+                    t.astype(f32).T[far - narrow :, :].astype(bf16)
+                )
+
+    @pl.when(side == 1)
+    def _():
+        for hi in range(2):
+            for hj in range(2):
+                t = y0[hj * half + wide : (hj + 1) * half, hi * half : hi * half + wide]
+                y0[hi * half : hi * half + far, hj * half + wide : (hj + 1) * half] = (
+                    t.astype(f32).T[:far, :].astype(bf16)
+                )
+
+    for q in range(members):
+        at = slice(q * rows, (q + 1) * rows)
+        ids = q * rows + lax.broadcasted_iota(jnp.int32, (rows, order), 0)
         eye = ids == lax.broadcasted_iota(jnp.int32, (rows, order), 1)
         z1[at, :] = ((jnp.where(eye, 3.0, 0.0) - y0[at, :].astype(f32)) * 0.5).astype(bf16)
-
-    forwards = []
-    for k in range(reps):
-        src = lax.rem(rep - k + reps, reps)
-        if k:
-            ins[k - 1].wait_recv()
-        at = block_rows(blk, src)
-        copy = remote(y0.at[at], y0.at[at], fwd_send.at[k], fwd_recv.at[k], rep, 1 - blk)
-        copy.start()
-        forwards.append(copy)
-        first_step(blk, src)
-    for k in range(reps):
-        src = lax.rem(rep - k + reps, reps)
-        forwards[k].wait_recv()
-        first_step(1 - blk, src)
 
     mine = pl.ds(pl.multiple_of(blk * half, half), half)
     pending = []
@@ -164,40 +217,47 @@
         slot, ex = slot + 2, ex + 2
     make_step(y, z, z_in)
 
+    for n in range(chunks):
+        z1[0:half, cols(n)] = product(step[...], z, None, n).astype(bf16)
+
+    def local_rows(r):
+        return pl.ds(pl.multiple_of(r * rows, rows), rows)
+
+    invs = []
+    for k in range(1, reps):
+        p = target(k)
+        copy = remote(
+            z1.at[local_rows(p)], inv_ref.at[rep], inv_send.at[k], inv_recv.at[k], p, blk
+        )
+        copy.start()
+        invs.append(copy)
+
     my_cols = pl.ds(pl.multiple_of(blk * half, LANES), half)
     for n in range(chunks):
         out = product(step[...], y, y_in, n)
         last_root[cols(n), :] = out.T.astype(bf16)
     roots = []
-    for j in range(1, members):
-        r, b = member(j)
-        copy = remote(
-            last_root.at[block_rows(b, r)], root_ref.at[rep, :, my_cols],
-            root_send.at[j], root_recv.at[j], r, b,
-        )
-        copy.start()
-        roots.append(copy)
+    for k in list(range(1, reps)) + [0]:
+        for flip in range(2):
+            if k == 0 and flip == 0:
+                continue
+            r = target(k) if k else rep
+            b = blk + flip - 2 * blk * flip
+            copy = remote(
+                last_root.at[block_rows(b, r)], root_ref.at[rep, :, my_cols],
+                root_send.at[k, flip], root_recv.at[k, flip], r, b,
+            )
+            copy.start()
+            roots.append(copy)
+    inv_ref[rep] = z1[local_rows(rep), :]
     root_ref[rep, :, my_cols] = last_root[block_rows(blk, rep), :]
 
-    for n in range(chunks):
-        z1[0:half, cols(n)] = product(step[...], z, None, n).astype(bf16)
-
-    def local_rows(r):
-        return pl.ds(pl.multiple_of(r * rows, rows), rows)
-
-    invs = []
-    for k in range(1, reps):
-        p = lax.rem(rep + k, reps)
-        copy = remote(
-            z1.at[local_rows(p)], inv_ref.at[rep], inv_send.at[k], inv_recv.at[k], p, blk
-        )
-        copy.start()
-        invs.append(copy)
-    inv_ref[rep] = z1[local_rows(rep), :]
-
-    for copy in ins + forwards + pending:
+    for copies in ins:
+        for copy in copies:
+            copy.wait_send()
+    for copy in pending:
         copy.wait_send()
-    for copy in roots + invs:
+    for copy in invs + roots:
         copy.wait()
 
 
@@ -232,10 +292,10 @@
             pltpu.VMEM((order, half), jnp.bfloat16),
             dma((facs,)),
             dma((members,)), dma((members,)),
-            dma((reps,)), dma((reps,)),
-            dma((reps,)), dma((reps,)),
+            dma((reps, 2)), dma((reps, 2)),
+            dma((reps, 2)), dma((reps, 2)),
             dma((exchanges, chunks)), dma((exchanges, chunks)),
-            dma((members,)), dma((members,)),
+            dma((reps, 2)), dma((reps, 2)),
             dma((reps,)), dma((reps,)),
         ],
         compiler_params=pltpu.CompilerParams(
@@ -292,6 +352,8 @@
             facs == mesh.shape["rep"]
             and mesh.shape["blk"] == 2
             and rows % 16 == 0
+            and facs % 2 == 0
+            and (rows * facs) % LANES == 0
             and order % CHUNK == 0
         ):
             return fused(mesh, factors, damping)

time: 170 us -> 160 us (0.941)
  the two profiles are of different devices: /device:TPU:31 before, /device:TPU:0 now
where the time goes in v2:
time: 160 us; the launch traced here: 158 us
  Pallas kernels  151 us (94%)
  other arithmetic  5.48 us (3%)
    pallas_call x1, Pallas kernels, fused(): pl.pallas_call(functools.partial(kernel, reps), out_shape=(jax.ShapeDtype...  151 us
    div x1, other arithmetic, fused(): inv.astype(jnp.float32) / root_scale  5.48 us

profile of v2, /device:TPU:0, one launch (start us, length us, event | category | flops | bytes accessed | tf_op | source)
XLA Modules:
  0.0 158.2 jit_solution(15290434719024504219)
XLA Ops:
  0.6 151.3 %shard_map.41 = (bf16[8,80,1280]{2,1,0:T(8,128)(2,1)}, bf16[8,80,1280]{2,1,0:T(8,128)(2,1)}, f32[8,128]{1,0:T(8,128)}) custom-call(f32[8,80,1280]{2,1,0:T(8,128)} %fac_hbm.1, f32[8]{0:T(128)} %damp_ref.1), custom_call_target="tpu_custom_call" | custom-call | tf_op jit(solution)/shard_map/pallas_call | solution.py:273
  151.9 0.8 sqrt_reduce_fusion
  152.7 5.5 %convert_divide_fusion = (f32[8,80,1280]{2,1,0:T(8,128)}, f32[8,80,1280]{2,1,0:T(8,128)}) fusion(bf16[8,80,1280]{2,1,0:T(8,128)(2,1)} %get-tuple-element.7, f32[8]{0:T(128)S(1)} %sqrt_reduce_fusion, bf16[8,80,1280]{2,1,0:T(8,128)(2,1)} %get-tuple-element.5), kind=kLoop, calls=%fused_computation | loop fusion | flops 3276800 | bytes 9830432 | tf_op jit(solution)/shard_map/div | solution.py:306

commit v3 on v2

--- a/solution.py
+++ b/solution.py
@@ -104,66 +104,105 @@
             return (1 - side) * side_reps + back
         return side * side_reps + back
 
-    def pieces(k, owner_side):
+    tiles = half // LANES
+    widths = sorted({tiles - (r * rows) // LANES for r in range(side_reps, reps)})
+
+    def width_of(r, owner_side):
+        mirrored = r + owner_side * (reps - 1 - 2 * r)
+        return tiles - (mirrored * rows) // LANES
+
+    def pieces(k, src, owner_side):
         if k == 0 or k > side_reps:
-            return [pl.ds(0, order)]
-        first = (1 - owner_side) * narrow
-        return [
-            pl.ds(pl.multiple_of(h * half + first, LANES), wide) for h in range(2)
-        ]
-
-    ins = []
+            return [(None, [pl.ds(0, order)])]
+        options = []
+        for w in widths:
+            first = (1 - owner_side) * (half - w * LANES)
+            options.append((
+                width_of(src, owner_side) == w,
+                [pl.ds(pl.multiple_of(h * half + first, LANES), w * LANES) for h in range(2)],
+            ))
+        return options
+
+    def each(options, act):
+        for condition, columns in options:
+            if condition is None:
+                act(columns)
+            else:
+                pl.when(condition)(functools.partial(act, columns))
+
+    own_rows = block_rows(blk, rep)
+
+    def in_copy(k, i, c):
+        return remote(
+            send_buf.at[k, :, c], y0.at[own_rows, c],
+            in_send.at[k, i], in_recv.at[k, i], target(k), blk,
+        )
+
+    def send_in(k, columns):
+        for i, c in enumerate(columns):
+            in_copy(k, i, c).start()
+
+    def wait_in(k, columns):
+        for i, c in enumerate(columns):
+            in_copy(k, i, c).wait_send()
+
     for k in range(1, reps):
         p = target(k)
         send_buf[k] = (damped(p) * scale[pl.ds(p, 1), 0:1]).astype(bf16)
-        at = block_rows(blk, rep)
-        copies = [
-            remote(
-                send_buf.at[k, :, c], y0.at[at, c],
-                in_send.at[k, i], in_recv.at[k, i], p, blk,
-            )
-            for i, c in enumerate(pieces(k, 1 - side))
-        ]
-        for copy in copies:
-            copy.start()
-        ins.append(copies)
-    y0[block_rows(blk, rep), :] = (damped(rep) * scale[pl.ds(rep, 1), 0:1]).astype(bf16)
-
-    forwards = []
+        each(pieces(k, rep, 1 - side), functools.partial(send_in, k))
+    y0[own_rows, :] = (damped(rep) * scale[pl.ds(rep, 1), 0:1]).astype(bf16)
+
+    def forward_copy(k, i, c):
+        at = block_rows(blk, source(k))
+        return remote(
+            y0.at[at, c], y0.at[at, c], fwd_send.at[k, i], fwd_recv.at[k, i], rep, 1 - blk
+        )
+
+    def forward(k, columns):
+        for i, c in enumerate(columns):
+            if k:
+                in_copy(k, i, c).wait_recv()
+            forward_copy(k, i, c).start()
+
+    def wait_forward(k, columns):
+        for i, c in enumerate(columns):
+            forward_copy(k, i, c).wait()
+
     for k in [0] + list(range(side_reps + 1, reps)) + list(range(1, side_reps + 1)):
-        at = block_rows(blk, source(k))
-        for i, c in enumerate(pieces(k, side)):
-            if k:
-                ins[k - 1][i].wait_recv()
-            copy = remote(
-                y0.at[at, c], y0.at[at, c], fwd_send.at[k, i], fwd_recv.at[k, i], rep, 1 - blk
-            )
-            copy.start()
-            forwards.append(copy)
-    for copy in forwards:
-        copy.wait_recv()
-    for copy in forwards:
-        copy.wait_send()
+        each(pieces(k, source(k), side), functools.partial(forward, k))
+    for k in range(reps):
+        each(pieces(k, source(k), side), functools.partial(wait_forward, k))
 
     far = half // 2
+    miss = half - min(widths) * LANES
+
+    def fill(t, old, row0, col0, mirrored):
+        shape = (far, miss)
+        r = (row0 + lax.broadcasted_iota(jnp.int32, shape, 0)) // rows
+        c = (col0 + lax.broadcasted_iota(jnp.int32, shape, 1)) // LANES
+        if mirrored:
+            gone = c >= tiles - ((reps - 1 - r) * rows) // LANES
+        else:
+            gone = c < (r * rows) // LANES
+        return jnp.where(gone, t, old.astype(f32)).astype(bf16)
 
     @pl.when(side == 0)
     def _():
         for hi in range(2):
             for hj in range(2):
-                t = y0[hj * half : hj * half + narrow, hi * half + narrow : (hi + 1) * half]
-                y0[hi * half + far : (hi + 1) * half, hj * half : hj * half + narrow] = (
-                    t.astype(f32).T[far - narrow :, :].astype(bf16)
-                )
+                t = y0[hj * half : hj * half + miss, hi * half + narrow : (hi + 1) * half]
+                at = (slice(hi * half + far, (hi + 1) * half), slice(hj * half, hj * half + miss))
+                t = t.astype(f32).T[far - narrow :, :]
+                y0[at] = fill(t, y0[at], far, 0, False)
 
     @pl.when(side == 1)
     def _():
         for hi in range(2):
             for hj in range(2):
-                t = y0[hj * half + wide : (hj + 1) * half, hi * half : hi * half + wide]
-                y0[hi * half : hi * half + far, hj * half + wide : (hj + 1) * half] = (
-                    t.astype(f32).T[:far, :].astype(bf16)
-                )
+                t = y0[(hj + 1) * half - miss : (hj + 1) * half, hi * half : hi * half + wide]
+                at = (slice(hi * half, hi * half + far), slice((hj + 1) * half - miss, (hj + 1) * half))
+                t = t.astype(f32).T[:far, :]
+                y0[at] = fill(t, y0[at], 0, half - miss, True)
 
     for q in range(members):
         at = slice(q * rows, (q + 1) * rows)
@@ -252,9 +291,8 @@
     inv_ref[rep] = z1[local_rows(rep), :]
     root_ref[rep, :, my_cols] = last_root[block_rows(blk, rep), :]
 
-    for copies in ins:
-        for copy in copies:
-            copy.wait_send()
+    for k in range(1, reps):
+        each(pieces(k, rep, 1 - side), functools.partial(wait_in, k))
     for copy in pending:
         copy.wait_send()
     for copy in invs + roots:

time: 160 us -> 155 us (0.969)
  Pallas kernels: 151 us -> 148 us
    pallas_call x1, Pallas kernels: 151 us -> 148 us  [fused(): pl.pallas_call(functools.partial(kernel, reps), out_shape=(jax.ShapeDtype...]
where the time goes in v3:
time: 155 us; the launch traced here: 154 us
  Pallas kernels  148 us (95%)
  other arithmetic  5.48 us (4%)
    pallas_call x1, Pallas kernels, fused(): pl.pallas_call(functools.partial(kernel, reps), out_shape=(jax.ShapeDtype...  148 us
    div x1, other arithmetic, fused(): inv.astype(jnp.float32) / root_scale  5.48 us

profile of v3, /device:TPU:0, one launch (start us, length us, event | category | flops | bytes accessed | tf_op | source)
XLA Modules:
  0.0 154.4 jit_solution(11749190187257543410)
XLA Ops:
  0.6 147.5 %shard_map.41 = (bf16[8,80,1280]{2,1,0:T(8,128)(2,1)}, bf16[8,80,1280]{2,1,0:T(8,128)(2,1)}, f32[8,128]{1,0:T(8,128)}) custom-call(f32[8,80,1280]{2,1,0:T(8,128)} %fac_hbm.1, f32[8]{0:T(128)} %damp_ref.1), custom_call_target="tpu_custom_call" | custom-call | tf_op jit(solution)/shard_map/pallas_call | solution.py:311
  148.2 0.8 sqrt_reduce_fusion
  149.0 5.5 %convert_divide_fusion = (f32[8,80,1280]{2,1,0:T(8,128)}, f32[8,80,1280]{2,1,0:T(8,128)}) fusion(bf16[8,80,1280]{2,1,0:T(8,128)(2,1)} %get-tuple-element.7, f32[8]{0:T(128)S(1)} %sqrt_reduce_fusion, bf16[8,80,1280]{2,1,0:T(8,128)(2,1)} %get-tuple-element.5), kind=kLoop, calls=%fused_computation | loop fusion | flops 3276800 | bytes 9830432 | tf_op jit(solution)/shard_map/div | solution.py:344
